TPU v7x, 32 devices: a whole 2x2x4 slice. The times are simulated.
32 devices in a mesh: member: 2 (over core), section: 4 (over y, x), atoms: 4 (over z).
Axes of the slice: x: 2, y: 2, z: 4, core: 2. Of those that a mesh axis runs over, the one named last changes fastest.
Arguments:
- positions: float32 [8, 3, 512], P(None, None, 'atoms'), may hold values from -8 to 8
- atom_types: int32 [8, 512], P(None, 'atoms'), may hold values from 0 to 127
- neighbors: int32 [8, 512, 128], P(None, 'atoms'), may hold values from 0 to 511
- nbr_mask: int32 [8, 512, 128], P(None, 'atoms'), may hold values 0 or 1
- type_table: bfloat16 [2, 128, 128], P('member'), may hold values from -6 to 6
- norm_gain: bfloat16 [2, 4, 128], P('member', 'section'), may hold values from 0.25 to 1.75
- proj_weight: bfloat16 [2, 4, 128, 384], P('member', 'section'), may hold values from -0.5 to 0.5
- out_weight: bfloat16 [2, 4, 128, 128], P('member', 'section'), may hold values from -0.5 to 0.5
- force_coef: bfloat16 [2, 4, 4], P('member', 'section'), may hold values from -48 to 48
Outputs:
- atom_dev: float32 [8, 512], P('section', 'atoms')
- max_dev: float32 [8], P('section')
- mean_force: float32 [8, 3, 512], P('section', None, 'atoms')
Inputs may be any that keep to these rules, and one draw needn't show every extreme that they name: `neighbors`: indices of atoms of the same frame, repeats and the atom itself allowed.
All inputs are finite; a program needn't handle non-finite values. No bound on the sum of `nbr_mask` on one device may be relied on, other than what follows from the above.
Results may differ from a plain program's by a relative error of at most 0.013.
Values may be sent and summed in bfloat16 or wider, within the bound.
No kernel may reach another device: no remote copies, remote signals or barrier semaphores. Data moves between devices by JAX's collectives and lax.ppermute only.
A program may use at most 64 MiB of HBM per device.

v0:
```python
import math
import jax
import jax.numpy as jnp
from jax import lax
from jax.sharding import PartitionSpec as P


def geometry(nbr, mask, pos_all, pos_own):
    total_atoms = pos_all.shape[1]
    hit = (nbr[:, :, None] == lax.iota(jnp.int32, total_atoms)[None, None, :]).astype(jnp.float32)
    counts = jnp.sum(hit * mask.astype(jnp.float32)[:, :, None], 1)
    delta = pos_all[:, None, :] - pos_own[:, :, None]
    switch = 1.0 / (1.0 + 0.125 * jnp.sum(delta * delta, 0))
    return (counts * switch, delta)


def block_dev(h_in, gain, proj, outw, coef, pair, delta, slots):
    width = h_in.shape[1]
    heads = coef.shape[0]
    head_dim = width // heads
    count = h_in.shape[0]
    hf = h_in.astype(jnp.float32)
    normed = (
        hf * lax.rsqrt(jnp.mean(hf * hf, -1, keepdims=True) + 1e-06) * gain.astype(jnp.float32)
    ).astype(jnp.bfloat16)
    query = jnp.dot(normed, proj[:, :width], preferred_element_type=jnp.float32).astype(
        jnp.bfloat16
    )
    keyval = jnp.dot(
        lax.all_gather(normed, "atoms", axis=0, tiled=True),
        proj[:, width:],
        preferred_element_type=jnp.float32,
    ).astype(jnp.bfloat16)
    total_atoms = keyval.shape[0]
    query3 = query.reshape(count, heads, head_dim)
    keys = keyval[:, :width].reshape(total_atoms, heads, head_dim)
    values = keyval[:, width:].reshape(total_atoms, heads, head_dim)
    scores = jnp.einsum(
        "ahd,jhd->haj", query3, keys, preferred_element_type=jnp.float32
    ) / math.sqrt(head_dim)
    weights = jax.nn.sigmoid(scores) * pair[None]
    message = jnp.einsum(
        "haj,jhd->ahd", weights.astype(jnp.bfloat16), values, preferred_element_type=jnp.float32
    )
    message = (message / slots).reshape(count, width).astype(jnp.bfloat16)
    h_out = (hf + jnp.dot(message, outw, preferred_element_type=jnp.float32)).astype(jnp.bfloat16)
    pair_coef = jnp.einsum("h,haj->aj", coef.astype(jnp.float32), weights)
    force = jnp.einsum("aj,caj->ca", pair_coef, delta) / slots
    return (h_out, force)


def embed(types_now, table):
    onehot = (types_now[:, None] == lax.iota(jnp.int32, table.shape[0])[None, :]).astype(
        jnp.bfloat16
    )
    return jnp.dot(onehot, table, preferred_element_type=jnp.float32).astype(jnp.bfloat16)


def shards(
    positions,
    atom_types,
    neighbors,
    nbr_mask,
    type_table,
    norm_gain,
    proj_weight,
    out_weight,
    force_coef,
):
    n_section = lax.axis_size("section")
    section_idx = lax.axis_index("section")
    frames = atom_types.shape[0]
    per_section = frames // n_section
    count = atom_types.shape[1]
    slots = neighbors.shape[2]
    table = type_table[0]
    pos_all = lax.all_gather(positions, "atoms", axis=2, tiled=True)
    gains, projs, outs, coefs = (
        lax.all_gather(norm_gain, "section", axis=1, tiled=True),
        lax.all_gather(proj_weight, "section", axis=1, tiled=True),
        lax.all_gather(out_weight, "section", axis=1, tiled=True),
        lax.all_gather(force_coef, "section", axis=1, tiled=True),
    )
    first = section_idx * per_section

    def whole_frame(local, own_forces):
        frame = first + local
        nbr = lax.dynamic_index_in_dim(neighbors, frame, 0, keepdims=False)
        mask = lax.dynamic_index_in_dim(nbr_mask, frame, 0, keepdims=False)
        pos_now = lax.dynamic_index_in_dim(pos_all, frame, 0, keepdims=False)
        pos_own = lax.dynamic_index_in_dim(positions, frame, 0, keepdims=False)
        pair, delta = geometry(nbr, mask, pos_now, pos_own)
        h_cur = embed(lax.dynamic_index_in_dim(atom_types, frame, 0, keepdims=False), table)
        total = jnp.zeros((3, count), jnp.float32)
        for blk in range(n_section):
            h_cur, term = block_dev(
                h_cur, gains[0, blk], projs[0, blk], outs[0, blk], coefs[0, blk], pair, delta, slots
            )
            total = total + term
        return lax.dynamic_update_index_in_dim(own_forces, total, local, 0)

    own = lax.fori_loop(
        0, per_section, whole_frame, jnp.zeros((per_section, 3, count), jnp.float32)
    )
    members = lax.axis_size("member")
    mean_force = lax.psum(own, "member") / members
    centered = own - mean_force
    spread = lax.psum(jnp.sum(centered * centered, 1), "member") / members
    atom_dev = jnp.sqrt(spread)
    max_dev = lax.pmax(jnp.max(atom_dev, -1), "atoms")
    return (atom_dev, max_dev, mean_force)


def solution(mesh):
    return jax.shard_map(
        shards,
        mesh=mesh,
        in_specs=(
            P(None, None, "atoms"),
            P(None, "atoms"),
            P(None, "atoms", None),
            P(None, "atoms", None),
            P("member", None, None),
            P("member", "section", None),
            P("member", "section", None, None),
            P("member", "section", None, None),
            P("member", "section", None),
        ),
        out_specs=(P("section", "atoms"), P("section"), P("section", None, "atoms")),
        check_vma=False,
    )
```

profile of v0, /device:TPU:0, one launch (start us, length us, event | category | flops | bytes accessed | tf_op | source)
XLA Modules:
  0.0 200.3 jit_solution(8612434693529792498)
XLA Ops:
  0.6 9.5 %all_gather.44 = bf16[1,4,128]{2,0,1:T(2,128)(2,1)S(1)} all-gather(bf16[1,1,128]{2,0,1:T(2,128)(2,1)} %bitcast.301), channel_id=1, replica_groups=mesh['member'=2,'section'=4,'atoms'=4] {'section'}, dimensions={1}, use_global_device_ids=true | all-gather | bytes 1280 | tf_op jit(solution)/shard_map/all_gather | solution.py:79
  10.2 7.8 %all_gather.46 = bf16[1,4,4]{2,0,1:T(2,128)(2,1)S(1)} all-gather(bf16[1,1,4]{2,0,1:T(2,128)(2,1)} %bitcast.302), channel_id=1, replica_groups=mesh['member'=2,'section'=4,'atoms'=4] {'section'}, dimensions={1}, use_global_device_ids=true | all-gather | bytes 40 | tf_op jit(solution)/shard_map/all_gather | solution.py:82
  18.0 0.7 copy.31
  18.7 12.2 %all_gather.43 = f32[8,3,512]{2,1,0:T(4,128)S(1)} all-gather(f32[8,3,128]{2,1,0:T(4,128)S(1)} %copy.31), channel_id=1, replica_groups=mesh['member'=2,'section'=4,'atoms'=4] {'atoms'}, dimensions={2}, use_global_device_ids=true | all-gather | bytes 61440 | tf_op jit(solution)/shard_map/all_gather | solution.py:77
  30.9 7.7 %all_gather.47 = bf16[1,4,128,128]{3,2,0,1:T(8,128)(2,1)S(1)} all-gather(bf16[1,1,128,128]{3,2,0,1:T(8,128)(2,1)} %bitcast.300), channel_id=1, replica_groups=mesh['member'=2,'section'=4,'atoms'=4] {'section'}, dimensions={1}, use_global_device_ids=true | all-gather | bytes 163840 | tf_op jit(solution)/shard_map/all_gather | solution.py:81
  38.6 9.3 %all_gather.45 = bf16[1,4,128,384]{3,2,0,1:T(8,128)(2,1)S(1)} all-gather(bf16[1,1,128,384]{3,2,0,1:T(8,128)(2,1)} %bitcast.299), channel_id=1, replica_groups=mesh['member'=2,'section'=4,'atoms'=4] {'section'}, dimensions={1}, use_global_device_ids=true | all-gather | bytes 491520 | tf_op jit(solution)/shard_map/all_gather | solution.py:80
  47.9 137.4 %while.13 = (s32[]{:T(128)}, f32[2,3,128]{2,0,1:T(2,128)S(1)}, s32[]{:T(128)}, f32[8,3,512]{2,1,0:T(4,128)S(1)}, f32[8,3,128]{2,1,0:T(4,128)S(1)}, /*index=5*/s3...) while((s32[]{:T(128)}, f32[2,3,128]{2,0,1:T(2,128)S(1)}, ...), condition=%wide.region_7.8_spmd, body=%wide.region_0.7_spmd.sunk | while | flops 322554368 | bytes 20396256 | solution.py:102
  47.9 0.7 fusion.231
  49.0 0.9 convert_bitcast_fusion.2
  49.9 6.0 %select_reduce_fusion.2 = f32[128,512]{1,0:T(8,128)S(1)} fusion(f32[128,128]{1,0:T(8,128)S(1)} %get-tuple-element.420, s32[128,128]{1,0:T(8,128)S(1)} %get-tuple-element.421), kind=kLoop, calls=%fused_computation.clone.1 | loop fusion | flops 25100288 | bytes 393216 | tf_op jit(solution)/shard_map/while/body/eval_jaxpr/reduce_sum | solution.py:11
  55.8 12.3 %all_gather.52 = bf16[512,128]{0,1:T(8,128)(2,1)S(1)} all-gather(bf16[128,128]{0,1:T(8,128)(2,1)S(1)} %multiply_convert_fusion.8), channel_id=1, replica_groups=mesh['member'=2,'section'=4,'atoms'=4] {'atoms'}, dimensions={0}, use_global_device_ids=true | all-gather | bytes 163840 | tf_op jit(solution)/shard_map/while/body/eval_jaxpr/all_gather | solution.py:30
  71.6 12.3 %all_gather.53 = bf16[512,128]{0,1:T(8,128)(2,1)S(1)} all-gather(bf16[128,128]{0,1:T(8,128)(2,1)S(1)} %multiply_convert_fusion.9), channel_id=1, replica_groups=mesh['member'=2,'section'=4,'atoms'=4] {'atoms'}, dimensions={0}, use_global_device_ids=true | all-gather | bytes 163840 | tf_op jit(solution)/shard_map/while/body/eval_jaxpr/all_gather | solution.py:30
  86.8 12.3 %all_gather.54 = bf16[512,128]{0,1:T(8,128)(2,1)S(1)} all-gather(bf16[128,128]{0,1:T(8,128)(2,1)S(1)} %multiply_convert_fusion.10), channel_id=1, replica_groups=mesh['member'=2,'section'=4,'atoms'=4] {'atoms'}, dimensions={0}, use_global_device_ids=true | all-gather | bytes 163840 | tf_op jit(solution)/shard_map/while/body/eval_jaxpr/all_gather | solution.py:30
  101.9 12.5 %all_gather.55 = bf16[512,128]{0,1:T(8,128)(2,1)S(1)} all-gather(bf16[128,128]{0,1:T(8,128)(2,1)S(1)} %multiply_convert_fusion.11), channel_id=1, replica_groups=mesh['member'=2,'section'=4,'atoms'=4] {'atoms'}, dimensions={0}, use_global_device_ids=true | all-gather | bytes 163840 | tf_op jit(solution)/shard_map/while/body/eval_jaxpr/all_gather | solution.py:30
  116.5 0.7 fusion.231
  117.6 0.9 convert_bitcast_fusion.2
  118.5 6.0 %select_reduce_fusion.2 = f32[128,512]{1,0:T(8,128)S(1)} fusion(f32[128,128]{1,0:T(8,128)S(1)} %get-tuple-element.420, s32[128,128]{1,0:T(8,128)S(1)} %get-tuple-element.421), kind=kLoop, calls=%fused_computation.clone.1 | loop fusion | flops 25100288 | bytes 393216 | tf_op jit(solution)/shard_map/while/body/eval_jaxpr/reduce_sum | solution.py:11
  124.5 12.5 %all_gather.52 = bf16[512,128]{0,1:T(8,128)(2,1)S(1)} all-gather(bf16[128,128]{0,1:T(8,128)(2,1)S(1)} %multiply_convert_fusion.8), channel_id=1, replica_groups=mesh['member'=2,'section'=4,'atoms'=4] {'atoms'}, dimensions={0}, use_global_device_ids=true | all-gather | bytes 163840 | tf_op jit(solution)/shard_map/while/body/eval_jaxpr/all_gather | solution.py:30
  140.5 12.4 %all_gather.53 = bf16[512,128]{0,1:T(8,128)(2,1)S(1)} all-gather(bf16[128,128]{0,1:T(8,128)(2,1)S(1)} %multiply_convert_fusion.9), channel_id=1, replica_groups=mesh['member'=2,'section'=4,'atoms'=4] {'atoms'}, dimensions={0}, use_global_device_ids=true | all-gather | bytes 163840 | tf_op jit(solution)/shard_map/while/body/eval_jaxpr/all_gather | solution.py:30
  155.8 12.3 %all_gather.54 = bf16[512,128]{0,1:T(8,128)(2,1)S(1)} all-gather(bf16[128,128]{0,1:T(8,128)(2,1)S(1)} %multiply_convert_fusion.10), channel_id=1, replica_groups=mesh['member'=2,'section'=4,'atoms'=4] {'atoms'}, dimensions={0}, use_global_device_ids=true | all-gather | bytes 163840 | tf_op jit(solution)/shard_map/while/body/eval_jaxpr/all_gather | solution.py:30
  170.9 12.3 %all_gather.55 = bf16[512,128]{0,1:T(8,128)(2,1)S(1)} all-gather(bf16[128,128]{0,1:T(8,128)(2,1)S(1)} %multiply_convert_fusion.11), channel_id=1, replica_groups=mesh['member'=2,'section'=4,'atoms'=4] {'atoms'}, dimensions={0}, use_global_device_ids=true | all-gather | bytes 163840 | tf_op jit(solution)/shard_map/while/body/eval_jaxpr/all_gather | solution.py:30
  185.3 2.5 %psum.14 = f32[2,3,128]{2,0,1:T(2,128)S(1)} all-reduce(f32[2,3,128]{2,0,1:T(2,128)S(1)} %get-tuple-element.217), channel_id=1, replica_groups=mesh['member'=2,'section'=4,'atoms'=4] {'member'}, use_global_device_ids=true, to_apply=%region_8.9 | all-reduce | flops 768 | bytes 6144 | tf_op jit(solution)/shard_map/psum | solution.py:106
  188.3 2.4 %psum.15 = f32[2,128]{1,0:T(2,128)S(1)} all-reduce(f32[2,128]{1,0:T(2,128)S(1)} %get-tuple-element.285), channel_id=1, replica_groups=mesh['member'=2,'section'=4,'atoms'=4] {'member'}, use_global_device_ids=true, to_apply=%region_10.11 | all-reduce | flops 256 | bytes 2048 | tf_op jit(solution)/shard_map/psum | solution.py:108
  191.5 8.9 %pmax.7 = f32[2]{0:T(128)} all-reduce(f32[2]{0:T(128)S(1)} %get-tuple-element.283), channel_id=1, replica_groups=mesh['member'=2,'section'=4,'atoms'=4] {'atoms'}, use_global_device_ids=true, to_apply=%region_12.13 | all-reduce | flops 2 | bytes 16 | tf_op jit(solution)/shard_map/pmax | solution.py:110
  (121 shorter events, 24.3 us)
Async XLA Ops:
  0.6 47.2 %copy-start = (bf16[1,128,128]{2,1,0:T(8,128)(2,1)S(1)}, bf16[1,128,128]{2,1,0:T(8,128)(2,1)}, u32[]{:S(2)}) copy-start(bf16[1,128,128]{2,1,0:T(8,128)(2,1)} %param.15) | copy-start | bytes 98308
where the time goes:
time: 201 us; the launch traced here: 200 us
  blocking collectives  159 us (79%)
  matrix products  20.5 us (10%)
  other arithmetic  16.4 us (8%)
  local copies, waits for them, and re-layouts  3.21 us (2%)
    all_gather x8, blocking collectives, block_dev(): lax.all_gather(normed, 'atoms', axis=0, tiled=True)  98.7 us
    all_gather x1, blocking collectives, shards(): pos_all = lax.all_gather(positions, 'atoms', axis=2, tiled=True)  12.2 us
    reduce_sum x2, other arithmetic, geometry(): counts = jnp.sum(hit * mask.astype(jnp.float32)[:, :, None], 1)  11.9 us
    all_gather x1, blocking collectives, shards(): lax.all_gather(norm_gain, 'section', axis=1, tiled=True)  9.53 us
    all_gather x1, blocking collectives, shards(): lax.all_gather(proj_weight, 'section', axis=1, tiled=True)  9.27 us
    pmax x1, blocking collectives, shards(): max_dev = lax.pmax(jnp.max(atom_dev, -1), 'atoms')  8.87 us
    all_gather x1, blocking collectives, shards(): lax.all_gather(force_coef, 'section', axis=1, tiled=True)  7.81 us
    all_gather x1, blocking collectives, shards(): lax.all_gather(out_weight, 'section', axis=1, tiled=True)  7.68 us

commit v1 on v0

--- a/solution.py
+++ b/solution.py
@@ -74,7 +74,8 @@
     count = atom_types.shape[1]
     slots = neighbors.shape[2]
     table = type_table[0]
-    pos_all = lax.all_gather(positions, "atoms", axis=2, tiled=True)
+    parts = lax.all_gather(positions, "atoms", axis=0, tiled=False)
+    pos_all = jnp.concatenate(parts, axis=2)
     gains, projs, outs, coefs = (
         lax.all_gather(norm_gain, "section", axis=1, tiled=True),
         lax.all_gather(proj_weight, "section", axis=1, tiled=True),

time: 201 us -> 203 us (level)
  no operation moved by 1% of the time
where the time goes in v1:
time: 203 us
  blocking collectives  160 us (79%)
  matrix products  20.5 us (10%)
  other arithmetic  16.4 us (8%)
  local copies, waits for them, and re-layouts  3.97 us (2%)
    all_gather x8, blocking collectives, block_dev(): lax.all_gather(normed, 'atoms', axis=0, tiled=True)  98.6 us
    all_gather x1, blocking collectives, shards(): parts = lax.all_gather(positions, 'atoms', axis=0, tiled=False)  13.6 us
    reduce_sum x2, other arithmetic, geometry(): counts = jnp.sum(hit * mask.astype(jnp.float32)[:, :, None], 1)  11.9 us
    all_gather x1, blocking collectives, shards(): lax.all_gather(norm_gain, 'section', axis=1, tiled=True)  9.66 us
    all_gather x1, blocking collectives, shards(): lax.all_gather(proj_weight, 'section', axis=1, tiled=True)  9.29 us
    pmax x1, blocking collectives, shards(): max_dev = lax.pmax(jnp.max(atom_dev, -1), 'atoms')  8.87 us
    all_gather x1, blocking collectives, shards(): lax.all_gather(force_coef, 'section', axis=1, tiled=True)  7.81 us
    all_gather x1, blocking collectives, shards(): lax.all_gather(out_weight, 'section', axis=1, tiled=True)  7.69 us

profile of v1, /device:TPU:0, one launch (start us, length us, event | category | flops | bytes accessed | tf_op | source)
XLA Modules:
  0.0 202.6 jit_solution(5075335206706424555)
XLA Ops:
  0.7 9.7 %all_gather.48 = bf16[1,4,128]{2,0,1:T(2,128)(2,1)S(1)} all-gather(bf16[1,1,128]{2,0,1:T(2,128)(2,1)} %bitcast.315), channel_id=1, replica_groups=mesh['member'=2,'section'=4,'atoms'=4] {'section'}, dimensions={1}, use_global_device_ids=true | all-gather | bytes 1280 | tf_op jit(solution)/shard_map/all_gather | solution.py:80
  10.3 7.8 %all_gather.50 = bf16[1,4,4]{2,0,1:T(2,128)(2,1)S(1)} all-gather(bf16[1,1,4]{2,0,1:T(2,128)(2,1)} %bitcast.316), channel_id=1, replica_groups=mesh['member'=2,'section'=4,'atoms'=4] {'section'}, dimensions={1}, use_global_device_ids=true | all-gather | bytes 40 | tf_op jit(solution)/shard_map/all_gather | solution.py:83
  18.1 13.6 %all-gather = f32[32,3,128]{2,0,1:T(8,128)S(1)} all-gather(f32[8,3,128]{2,0,1:T(8,128)} %param.11), channel_id=2, replica_groups=mesh['member'=2,'section'=4,'atoms'=4] {'atoms'}, dimensions={0}, use_global_device_ids=true | all-gather | bytes 61440 | tf_op jit(solution)/shard_map/all_gather | solution.py:77
  31.8 7.7 %all_gather.51 = bf16[1,4,128,128]{3,2,0,1:T(8,128)(2,1)S(1)} all-gather(bf16[1,1,128,128]{3,2,0,1:T(8,128)(2,1)} %bitcast.314), channel_id=1, replica_groups=mesh['member'=2,'section'=4,'atoms'=4] {'section'}, dimensions={1}, use_global_device_ids=true | all-gather | bytes 163840 | tf_op jit(solution)/shard_map/all_gather | solution.py:82
  39.5 9.3 %all_gather.49 = bf16[1,4,128,384]{3,2,0,1:T(8,128)(2,1)S(1)} all-gather(bf16[1,1,128,384]{3,2,0,1:T(8,128)(2,1)S(1)} %bitcast.313), channel_id=1, replica_groups=mesh['member'=2,'section'=4,'atoms'=4] {'section'}, dimensions={1}, use_global_device_ids=true | all-gather | bytes 491520 | tf_op jit(solution)/shard_map/all_gather | solution.py:81
  48.7 138.8 %while.13 = (s32[]{:T(128)}, f32[2,3,128]{2,0,1:T(2,128)S(1)}, s32[]{:T(128)}, f32[8,3,512]{2,0,1:T(8,128)S(1)}, f32[8,3,128]{2,0,1:T(8,128)}, /*index=5*/s32[8,...) while((s32[]{:T(128)}, f32[2,3,128]{2,0,1:T(2,128)S(1)}, ...), condition=%wide.region_7.8_spmd, body=%wide.region_0.7_spmd.sunk | while | flops 322554368 | bytes 20411616 | solution.py:103
  48.8 0.7 fusion.231
  49.5 0.7 constant_dynamic-slice_fusion.5
  50.6 0.9 convert_bitcast_fusion.2
  51.5 6.0 %select_reduce_fusion.2 = f32[128,512]{1,0:T(8,128)S(1)} fusion(f32[128,128]{1,0:T(8,128)S(1)} %get-tuple-element.420, s32[128,128]{1,0:T(8,128)S(1)} %get-tuple-element.421), kind=kLoop, calls=%fused_computation.clone.1 | loop fusion | flops 25100288 | bytes 393216 | tf_op jit(solution)/shard_map/while/body/eval_jaxpr/reduce_sum | solution.py:11
  57.4 12.3 %all_gather.56 = bf16[512,128]{0,1:T(8,128)(2,1)S(1)} all-gather(bf16[128,128]{0,1:T(8,128)(2,1)S(1)} %multiply_convert_fusion.8), channel_id=1, replica_groups=mesh['member'=2,'section'=4,'atoms'=4] {'atoms'}, dimensions={0}, use_global_device_ids=true | all-gather | bytes 163840 | tf_op jit(solution)/shard_map/while/body/eval_jaxpr/all_gather | solution.py:30
  73.2 12.3 %all_gather.57 = bf16[512,128]{0,1:T(8,128)(2,1)S(1)} all-gather(bf16[128,128]{0,1:T(8,128)(2,1)S(1)} %multiply_convert_fusion.9), channel_id=1, replica_groups=mesh['member'=2,'section'=4,'atoms'=4] {'atoms'}, dimensions={0}, use_global_device_ids=true | all-gather | bytes 163840 | tf_op jit(solution)/shard_map/while/body/eval_jaxpr/all_gather | solution.py:30
  88.4 12.3 %all_gather.58 = bf16[512,128]{0,1:T(8,128)(2,1)S(1)} all-gather(bf16[128,128]{0,1:T(8,128)(2,1)S(1)} %multiply_convert_fusion.10), channel_id=1, replica_groups=mesh['member'=2,'section'=4,'atoms'=4] {'atoms'}, dimensions={0}, use_global_device_ids=true | all-gather | bytes 163840 | tf_op jit(solution)/shard_map/while/body/eval_jaxpr/all_gather | solution.py:30
  103.6 12.4 %all_gather.59 = bf16[512,128]{0,1:T(8,128)(2,1)S(1)} all-gather(bf16[128,128]{0,1:T(8,128)(2,1)S(1)} %multiply_convert_fusion.11), channel_id=1, replica_groups=mesh['member'=2,'section'=4,'atoms'=4] {'atoms'}, dimensions={0}, use_global_device_ids=true | all-gather | bytes 163840 | tf_op jit(solution)/shard_map/while/body/eval_jaxpr/all_gather | solution.py:30
  118.8 0.7 constant_dynamic-slice_fusion.5
  119.9 0.9 convert_bitcast_fusion.2
  120.8 6.0 %select_reduce_fusion.2 = f32[128,512]{1,0:T(8,128)S(1)} fusion(f32[128,128]{1,0:T(8,128)S(1)} %get-tuple-element.420, s32[128,128]{1,0:T(8,128)S(1)} %get-tuple-element.421), kind=kLoop, calls=%fused_computation.clone.1 | loop fusion | flops 25100288 | bytes 393216 | tf_op jit(solution)/shard_map/while/body/eval_jaxpr/reduce_sum | solution.py:11
  126.7 12.3 %all_gather.56 = bf16[512,128]{0,1:T(8,128)(2,1)S(1)} all-gather(bf16[128,128]{0,1:T(8,128)(2,1)S(1)} %multiply_convert_fusion.8), channel_id=1, replica_groups=mesh['member'=2,'section'=4,'atoms'=4] {'atoms'}, dimensions={0}, use_global_device_ids=true | all-gather | bytes 163840 | tf_op jit(solution)/shard_map/while/body/eval_jaxpr/all_gather | solution.py:30
  142.5 12.6 %all_gather.57 = bf16[512,128]{0,1:T(8,128)(2,1)S(1)} all-gather(bf16[128,128]{0,1:T(8,128)(2,1)S(1)} %multiply_convert_fusion.9), channel_id=1, replica_groups=mesh['member'=2,'section'=4,'atoms'=4] {'atoms'}, dimensions={0}, use_global_device_ids=true | all-gather | bytes 163840 | tf_op jit(solution)/shard_map/while/body/eval_jaxpr/all_gather | solution.py:30
  158.0 12.3 %all_gather.58 = bf16[512,128]{0,1:T(8,128)(2,1)S(1)} all-gather(bf16[128,128]{0,1:T(8,128)(2,1)S(1)} %multiply_convert_fusion.10), channel_id=1, replica_groups=mesh['member'=2,'section'=4,'atoms'=4] {'atoms'}, dimensions={0}, use_global_device_ids=true | all-gather | bytes 163840 | tf_op jit(solution)/shard_map/while/body/eval_jaxpr/all_gather | solution.py:30
  173.2 12.3 %all_gather.59 = bf16[512,128]{0,1:T(8,128)(2,1)S(1)} all-gather(bf16[128,128]{0,1:T(8,128)(2,1)S(1)} %multiply_convert_fusion.11), channel_id=1, replica_groups=mesh['member'=2,'section'=4,'atoms'=4] {'atoms'}, dimensions={0}, use_global_device_ids=true | all-gather | bytes 163840 | tf_op jit(solution)/shard_map/while/body/eval_jaxpr/all_gather | solution.py:30
  187.5 2.5 %psum.14 = f32[2,3,128]{2,0,1:T(2,128)S(1)} all-reduce(f32[2,3,128]{2,0,1:T(2,128)S(1)} %get-tuple-element.217), channel_id=1, replica_groups=mesh['member'=2,'section'=4,'atoms'=4] {'member'}, use_global_device_ids=true, to_apply=%region_8.9 | all-reduce | flops 768 | bytes 6144 | tf_op jit(solution)/shard_map/psum | solution.py:107
  190.6 2.4 %psum.15 = f32[2,128]{1,0:T(2,128)S(1)} all-reduce(f32[2,128]{1,0:T(2,128)S(1)} %get-tuple-element.285), channel_id=1, replica_groups=mesh['member'=2,'section'=4,'atoms'=4] {'member'}, use_global_device_ids=true, to_apply=%region_10.11 | all-reduce | flops 256 | bytes 2048 | tf_op jit(solution)/shard_map/psum | solution.py:109
  193.7 8.9 %pmax.7 = f32[2]{0:T(128)} all-reduce(f32[2]{0:T(128)S(1)} %get-tuple-element.283), channel_id=1, replica_groups=mesh['member'=2,'section'=4,'atoms'=4] {'atoms'}, use_global_device_ids=true, to_apply=%region_12.13 | all-reduce | flops 2 | bytes 16 | tf_op jit(solution)/shard_map/pmax | solution.py:111
  (128 shorter events, 25.0 us)
Async XLA Ops:
  0.6 38.8 %copy-start.1 = (bf16[1,1,128,384]{3,2,1,0:T(8,128)(2,1)S(1)}, bf16[1,1,128,384]{3,2,1,0:T(8,128)(2,1)}, u32[]{:S(2)}) copy-start(bf16[1,1,128,384]{3,2,1,0:T(8,128)(2,1)} %param.17) | copy-start | bytes 294916
  0.6 48.1 %copy-start = (bf16[1,128,128]{2,1,0:T(8,128)(2,1)S(1)}, bf16[1,128,128]{2,1,0:T(8,128)(2,1)}, u32[]{:S(2)}) copy-start(bf16[1,128,128]{2,1,0:T(8,128)(2,1)} %param.15) | copy-start | bytes 98308
